TPU v7x, 32 devices: a whole 2x2x4 slice. The times are simulated.
32 devices in a mesh: task: 2 (over x), dp: 8 (over z, core), mp: 2 (over y).
Axes of the slice: x: 2, y: 2, z: 4, core: 2. Of those that a mesh axis runs over, the one named last changes fastest.
Arguments:
- deltas: bfloat16 [6, 2048, 4608], P('task', 'dp', 'mp'), may hold values from -400 to 400, as said below
- fishers: bfloat16 [6, 2048, 4608], P('task', 'dp', 'mp'), may hold values from 0.0009994507 to 1
Outputs:
- merged_out: float32 [2048, 4608], P('dp', 'mp')
Inputs may be any that keep to these rules, and one draw needn't show every extreme that they name: `deltas`: Real-valued weight differences.
All inputs are finite; a program needn't handle non-finite values.
Results may differ from a plain program's by a relative error of at most 0.0003.
Values sent between devices are 32-bit elements; how exact they have to be, the bound alone decides.
A program may use at most 64 MiB of HBM per device.

v0:
```python
import jax
import jax.numpy as jnp
from jax import lax
from jax.sharding import PartitionSpec as P


def task_squares(deltas):
    widened = deltas.astype(jnp.float32)
    own_sums = jnp.sum(widened * widened, axis=(1, 2))
    held_tasks = deltas.shape[0]
    slot_sums = jnp.zeros((held_tasks * lax.axis_size("task"),), jnp.float32)
    return lax.dynamic_update_slice(slot_sums, own_sums, (lax.axis_index("task") * held_tasks,))


def shards(deltas, fishers):
    weights = fishers.astype(jnp.float32)
    numerator = jnp.sum(weights * deltas.astype(jnp.float32), axis=0)
    denominator = jnp.sum(weights, axis=0)
    task_part = task_squares(deltas)
    task_sq = lax.psum(task_part, ("task", "dp", "mp"))
    numerator, denominator = (
        lax.psum_scatter(numerator, "task", scatter_dimension=0, tiled=True),
        lax.psum_scatter(denominator, "task", scatter_dimension=0, tiled=True),
    )
    half_rows = numerator / denominator
    merged_part = jnp.sum(half_rows * half_rows)
    merged = lax.all_gather(half_rows, "task", axis=0, tiled=True)
    merged_sq = lax.psum(merged_part, ("task", "dp", "mp"))
    target = jnp.mean(jnp.sqrt(task_sq + 1e-06))
    rescale = target / jnp.sqrt(merged_sq + 1e-06)
    return rescale * merged


def solution(mesh):
    placed = (P("task", "dp", "mp"), P("task", "dp", "mp"))
    return jax.shard_map(
        shards, mesh=mesh, in_specs=placed, out_specs=P("dp", "mp"), check_vma=False
    )
```

profile of v0, /device:TPU:0, one launch (start us, length us, event | category | flops | bytes accessed | tf_op | source)
XLA Modules:
  0.0 144.6 jit_solution(8158411460100088740)
XLA Ops:
  6.5 0.0 reduce-scatter.3.cloned.1.call-start
  6.5 7.8 %fusion = (f32[3]{0:T(128)S(1)}, f32[256,2304]{1,0:T(8,128)}, f32[256,2304]{1,0:T(8,128)}) fusion(bf16[3,256,2304]{2,1,0:T(8,128)(2,1)} %param.2, bf16[3,256,2304]{2,1,0:T(8,128)(2,1)} %param.3), kind=kLoop, calls=%fused_computation.3 | loop fusion | flops 11206653 | bytes 11796492 | tf_op jit(solution)/shard_map/reduce_sum | solution.py:9
  14.4 0.0 reduce-scatter.3.cloned.1.call-update
  14.4 0.0 reduce-scatter.5.cloned.1.call-start
  14.4 0.7 reduce-scatter.5.cloned.1.call-update
  15.1 0.0 all-gather.2.cloned.1.call-start
  15.2 36.9 %reduce-scatter.3.cloned.1.call-done = f32[128,2304]{1,0:T(8,128)} async-done(((f32[256,2304]{1,0:T(8,128)}), f32[128,2304]{1,0:T(8,128)}) %reduce-scatter.3.cloned.1.call-update) | async-done | bytes 1179664 | tf_op jit(solution)/shard_map/reduce_scatter | solution.py:22
  52.1 37.0 %reduce-scatter.5.cloned.1.call-done = f32[128,2304]{1,0:T(8,128)} async-done(((f32[256,2304]{1,0:T(8,128)}), f32[128,2304]{1,0:T(8,128)}) %reduce-scatter.5.cloned.1.call-update) | async-done | bytes 1179664 | tf_op jit(solution)/shard_map/reduce_scatter | solution.py:23
  89.1 3.5 %multiply_reduce_fusion = (f32[]{:T(128)}, f32[128,2304]{1,0:T(8,128)}) fusion(f32[128,2304]{1,0:T(8,128)} %reduce-scatter.3.cloned.1.call-done, f32[128,2304]{1,0:T(8,128)} %reduce-scatter.5.cloned.1.call-done), kind=kLoop, calls=%fused_computation.6 | loop fusion | flops 884735 | bytes 3538948 | tf_op jit(solution)/shard_map/reduce_sum | solution.py:26
  92.6 0.0 all-gather.2.cloned.1.call-update
  92.6 0.2 dynamic_update_slice.3
  92.9 40.1 %all-reduce = (f32[6]{0:T(128)S(1)}, f32[]{:T(128)}) all-reduce(f32[6]{0:T(128)S(1)} %dynamic_update_slice.3, f32[]{:T(128)} %get-tuple-element.10), channel_id=1, replica_groups=mesh['task'=2,'dp'=8,'mp'=2] {'task','dp','mp'}, use_global_device_ids=true, to_apply=%region_1.0 | all-reduce | flops 7 | bytes 56 | tf_op jit(solution)/shard_map/psum | solution.py:20
  133.7 0.6 sqrt_reduce_fusion
  134.8 0.0 all-gather.2.cloned.1.call-done
  134.9 3.2 %broadcast_multiply_fusion = f32[256,2304]{1,0:T(8,128)} fusion(f32[256,2304]{1,0:T(8,128)} %all-gather.2.cloned.1.call-done, f32[]{:T(128)S(6)} %div.11), kind=kLoop, calls=%fused_computation.5 | loop fusion | flops 589824 | bytes 4718596 | tf_op jit(solution)/shard_map/mul | solution.py:31
  (1 shorter events, 0.0 us)
Async XLA Ops:
  6.5 45.5 %reduce-scatter.3.cloned.1.call-start = ((), (), s32[]{:S(2)}) async-start(), calls=%async_computation.2 | async-start | bytes 3538944 | tf_op jit(solution)/shard_map/reduce_scatter | solution.py:22
  14.4 74.7 %reduce-scatter.5.cloned.1.call-start = ((), (), s32[]{:S(2)}) async-start(), calls=%async_computation.3 | async-start | bytes 3538944 | tf_op jit(solution)/shard_map/reduce_scatter | solution.py:23
  15.1 119.7 %all-gather.2.cloned.1.call-start = ((), (), s32[]{:S(2)}) async-start(), calls=%async_computation.4 | async-start | bytes 3538944 | tf_op jit(solution)/shard_map/all_gather | solution.py:27
Sparse Core Ops, SparseCore 0:
  14.5 37.5 reduce-scatter.2
  54.3 34.7 reduce-scatter.4
  92.7 36.3 all-gather.1
where the time goes:
time: 145 us
  waiting for transfers between devices  74.7 us (52%)
  blocking collectives  40.1 us (28%)
  other arithmetic  15.1 us (10%)
  between operations  14.4 us (10%)
    psum x1, blocking collectives, shards(): task_sq = lax.psum(task_part, ('task', 'dp', 'mp'))  40.1 us
    reduce_scatter x1, waiting for transfers between devices, shards(): lax.psum_scatter(denominator, 'task', scatter_dimension=0, tiled=True)  37 us
    reduce_scatter x1, waiting for transfers between devices, shards(): lax.psum_scatter(numerator, 'task', scatter_dimension=0, tiled=True)  36.9 us
    reduce_sum x1, other arithmetic, task_squares(): own_sums = jnp.sum(widened * widened, axis=(1, 2))  7.82 us
    reduce_sum x1, other arithmetic, shards(): merged_part = jnp.sum(half_rows * half_rows)  3.47 us
    mul x1, other arithmetic, shards(): return rescale * merged  3.23 us
  transfers between devices with their start and end apart: 3, of which 2 were waited for; matrix products, arithmetic and copies ran while one was open for 1% of the time, Pallas kernels for 0%

commit v1 on v0

v1 whole, which is shorter than its diff:
```python
import functools

import jax
import jax.numpy as jnp
from jax import lax
from jax.experimental import pallas as pl
from jax.experimental.pallas import tpu as pltpu
from jax.sharding import PartitionSpec as P

MESH = pl.DeviceIdType.MESH
ROW_STEP = 16
COL_STEP = 256
EARLY_REPLIES = 2


def exchange_steps(mesh):
    steps = []
    for axis in ("task", "mp", "dp"):
        size = mesh.shape[axis]
        assert size & (size - 1) == 0
        bit = 1
        while bit < size:
            steps.append((axis, bit))
            bit *= 2
    return steps


def peer_of(axis, bit):
    me = lax.axis_index(axis)
    return me + bit - 2 * bit * (me // bit % 2)


def kernel(steps, tasks, deltas, fishers, out, delta_v, fisher_v, sent, own, landed, merged, reply,
           staged, squares, merged_squares, sums, sums_in, load_sem, send_sem, recv_sem, reply_send, reply_recv,
           sum_send, sum_recv, store_sem):
    held, rows, cols = delta_v.shape
    half = rows // 2
    pieces = half // ROW_STEP
    me = lax.axis_index("task")
    partner = {"task": peer_of("task", 1)}
    mine_base = me * half
    other_base = (1 - me) * half
    blocks = [(at, min(COL_STEP, cols - at)) for at in range(0, cols, COL_STEP)]

    def row_at(base, c):
        return pl.ds(pl.multiple_of(base + c * ROW_STEP, ROW_STEP), ROW_STEP)

    def load(side, c):
        at = row_at(other_base if side == 0 else mine_base, c)
        return (
            pltpu.make_async_copy(deltas.at[:, at, :], delta_v.at[:, at, :], load_sem.at[side, 0, c]),
            pltpu.make_async_copy(fishers.at[:, at, :], fisher_v.at[:, at, :], load_sem.at[side, 1, c]),
        )

    def send(c):
        return pltpu.make_async_remote_copy(
            src_ref=sent.at[c], dst_ref=landed.at[c], send_sem=send_sem.at[c], recv_sem=recv_sem.at[c],
            device_id=partner, device_id_type=MESH)

    def answer(c):
        return pltpu.make_async_remote_copy(
            src_ref=merged.at[c], dst_ref=reply.at[c], send_sem=reply_send.at[c], recv_sem=reply_recv.at[c],
            device_id=partner, device_id_type=MESH)

    def exchange(s):
        axis, bit = steps[s]
        return pltpu.make_async_remote_copy(
            src_ref=sums.at[s], dst_ref=sums_in.at[s], send_sem=sum_send.at[s], recv_sem=sum_recv.at[s],
            device_id={axis: peer_of(axis, bit)}, device_id_type=MESH)

    def store(base, c):
        at = row_at(base, c)
        return pltpu.make_async_copy(staged.at[at, :], out.at[at, :], store_sem.at[base // half, c])

    for side in range(2):
        @pl.loop(0, pieces)
        def _(c):
            for copy in load(side, c):
                copy.start()

    barrier = pltpu.get_barrier_semaphore()
    for axis, bit in steps:
        pl.semaphore_signal(barrier, inc=1, device_id={axis: peer_of(axis, bit)}, device_id_type=MESH)

    squares[...] = jnp.zeros_like(squares)
    merged_squares[...] = jnp.zeros_like(merged_squares)

    def partial(side, c, target):
        for copy in load(side, c):
            copy.wait()
        at = row_at(other_base if side == 0 else mine_base, c)
        for start, width in blocks:
            span = pl.ds(start, width)
            numerator = denominator = None
            for k in range(held):
                weight = fisher_v[k, at, span].astype(jnp.float32)
                value = delta_v[k, at, span].astype(jnp.float32)
                squares[k, :, span] += value * value
                numerator = weight * value if k == 0 else numerator + weight * value
                denominator = weight if k == 0 else denominator + weight
            target[c, 0, :, span] = numerator
            target[c, 1, :, span] = denominator

    partial(0, 0, sent)
    pl.semaphore_wait(barrier, len(steps))

    @pl.loop(1, pieces)
    def _(c):
        partial(0, c, sent)
        send(c - 1).start()

    partial(1, 0, own)
    send(pieces - 1).start()

    @pl.loop(1, pieces)
    def _(c):
        partial(1, c, own)

    def merge(c):
        send(c).wait_recv()
        for start, width in blocks:
            span = pl.ds(start, width)
            value = (own[c, 0, :, span] + landed[c, 0, :, span]) / (own[c, 1, :, span] + landed[c, 1, :, span])
            merged[c, :, span] = value
            merged_squares[:, span] += value * value

    merge(0)

    @pl.loop(1, pieces)
    def _(c):
        merge(c)

        @pl.when(c <= EARLY_REPLIES)
        def _():
            answer(c - 1).start()

    index = lax.broadcasted_iota(jnp.int32, sums.shape[1:], 0)
    totals = jnp.where(index == tasks, jnp.sum(merged_squares[...]), 0.0)
    for k in range(held):
        totals = jnp.where(index == me * held + k, jnp.sum(squares[k]), totals)
    for s in range(len(steps)):
        sums[s] = totals
        exchange(s).start()
        if s == 0:
            @pl.loop(EARLY_REPLIES, pieces)
            def _(c):
                answer(c).start()
        exchange(s).wait_recv()
        totals = totals + sums_in[s]

    roots = jnp.sqrt(totals + 1e-06)
    target = jnp.sum(jnp.where(index < tasks, roots, 0.0), axis=0, keepdims=True) / tasks
    norm = jnp.sum(jnp.where(index == tasks, roots, 0.0), axis=0, keepdims=True)
    rescale = jnp.max(target / norm)

    @pl.loop(0, pieces)
    def _(c):
        at = row_at(mine_base, c)
        for start, width in blocks:
            span = pl.ds(start, width)
            staged[at, span] = merged[c, :, span] * rescale
        store(mine_base, c).start()

    @pl.loop(0, pieces)
    def _(c):
        answer(c).wait_recv()
        at = row_at(other_base, c)
        for start, width in blocks:
            span = pl.ds(start, width)
            staged[at, span] = reply[c, :, span] * rescale
        store(other_base, c).start()

    for s in range(len(steps)):
        exchange(s).wait_send()

    @pl.loop(0, pieces)
    def _(c):
        send(c).wait_send()
        answer(c).wait_send()
        store(mine_base, c).wait()
        store(other_base, c).wait()


def shards(mesh, deltas, fishers):
    held, rows, cols = deltas.shape
    assert mesh.shape["task"] == 2 and rows % (2 * ROW_STEP) == 0
    steps = exchange_steps(mesh)
    tasks = held * mesh.shape["task"]
    pieces = rows // 2 // ROW_STEP
    sum_rows = (tasks + 8) // 8 * 8
    f32 = jnp.float32
    dma = pltpu.SemaphoreType.DMA
    return pl.pallas_call(
        functools.partial(kernel, steps, tasks),
        out_shape=jax.ShapeDtypeStruct((rows, cols), f32),
        in_specs=[pl.BlockSpec(memory_space=pl.ANY)] * 2,
        out_specs=pl.BlockSpec(memory_space=pl.ANY),
        scratch_shapes=[
            pltpu.VMEM(deltas.shape, deltas.dtype),
            pltpu.VMEM(fishers.shape, fishers.dtype),
            pltpu.VMEM((pieces, 2, ROW_STEP, cols), f32),
            pltpu.VMEM((pieces, 2, ROW_STEP, cols), f32),
            pltpu.VMEM((pieces, 2, ROW_STEP, cols), f32),
            pltpu.VMEM((pieces, ROW_STEP, cols), f32),
            pltpu.VMEM((pieces, ROW_STEP, cols), f32),
            pltpu.VMEM((rows, cols), f32),
            pltpu.VMEM((held, ROW_STEP, cols), f32),
            pltpu.VMEM((ROW_STEP, cols), f32),
            pltpu.VMEM((len(steps), sum_rows, 128), f32),
            pltpu.VMEM((len(steps), sum_rows, 128), f32),
            dma((2, 2, pieces)),
            dma((pieces,)),
            dma((pieces,)),
            dma((pieces,)),
            dma((pieces,)),
            dma((len(steps),)),
            dma((len(steps),)),
            dma((2, pieces)),
        ],
        compiler_params=pltpu.CompilerParams(collective_id=0, has_side_effects=True),
        name="merge",
    )(deltas, fishers)


def solution(mesh):
    placed = (P("task", "dp", "mp"), P("task", "dp", "mp"))
    return jax.shard_map(
        functools.partial(shards, mesh), mesh=mesh, in_specs=placed, out_specs=P("dp", "mp"), check_vma=False
    )
```

time: 145 us -> 87 us (0.60)
  Pallas kernels: 0 us -> 83.6 us
  waiting for transfers between devices: 74.7 us -> 0 us
  blocking collectives: 40.1 us -> 0 us
  other arithmetic: 15.1 us -> 0 us
  between operations: 14.4 us -> 0.01 us
  local copies, waits for them, and re-layouts: 0.24 us -> 3.22 us
    pallas_call x0 -> x1, Pallas kernels: none -> 83.6 us  [shards(): pl.pallas_call(functools.partial(kernel, steps, tasks), out_shape=jax.Sha...]
    reduce_scatter x2 -> x0, waiting for transfers between devices: 73.9 us -> none  [the longest x1 37 us: shards(): lax.psum_scatter(denominator, 'task', scatter_dimension=0, tiled=True)]
    psum x1 -> x0, blocking collectives: 40.1 us -> none  [shards(): task_sq = lax.psum(task_part, ('task', 'dp', 'mp'))]
    reduce_sum x3 -> x0, other arithmetic: 11.9 us -> none  [the longest x1 7.82 us: task_squares(): own_sums = jnp.sum(widened * widened, axis=(1, 2))]
    mul x1 -> x0, other arithmetic: 3.23 us -> none  [shards(): return rescale * merged]
    unnamed x0 -> x1, local copies, waits for them, and re-layouts: none -> 3.22 us
  transfers between devices with their start and end apart: 3 -> 0, of which waited for: 2 -> 0; matrix products, arithmetic and copies ran while one was open for 1% -> 0% of each run, Pallas kernels for 0% -> 0%
where the time goes in v1:
time: 87 us; the launch traced here: 86.9 us
  Pallas kernels  83.6 us (96%)
  local copies, waits for them, and re-layouts  3.22 us (4%)
    pallas_call x1, Pallas kernels, shards(): pl.pallas_call(functools.partial(kernel, steps, tasks), out_shape=jax.Sha...  83.6 us
    unnamed x1, local copies, waits for them, and re-layouts  3.22 us

profile of v1, /device:TPU:0, one launch (start us, length us, event | category | flops | bytes accessed | tf_op | source)
XLA Modules:
  0.0 86.9 jit_solution(5520822608374229131)
XLA Ops:
  0.0 83.6 %merge.1 = f32[256,2304]{1,0:T(8,128)} custom-call(bf16[3,256,2304]{2,1,0:T(8,128)(2,1)} %deltas.1, bf16[3,256,2304]{2,1,0:T(8,128)(2,1)} %fishers.1), custom_call_target="tpu_custom_call" | custom-call | tf_op jit(solution)/shard_map/merge/pallas_call | solution.py:193
  83.7 3.2 %copy.4 = f32[256,2304]{1,0:T(8,128)} copy(f32[256,2304]{1,0:T(8,128)} %merge.1) | data formatting | bytes 4718592

commit v2 on v1

--- a/solution.py
+++ b/solution.py
@@ -31,8 +31,8 @@
 
 
 def kernel(steps, tasks, deltas, fishers, out, delta_v, fisher_v, sent, own, landed, merged, reply,
-           staged, squares, merged_squares, sums, sums_in, load_sem, send_sem, recv_sem, reply_send, reply_recv,
-           sum_send, sum_recv, store_sem):
+           squares, merged_squares, sums, sums_in, load_sem, send_sem, recv_sem, reply_send, reply_recv,
+           sum_send, sum_recv):
     held, rows, cols = delta_v.shape
     half = rows // 2
     pieces = half // ROW_STEP
@@ -68,19 +68,18 @@
             src_ref=sums.at[s], dst_ref=sums_in.at[s], send_sem=sum_send.at[s], recv_sem=sum_recv.at[s],
             device_id={axis: peer_of(axis, bit)}, device_id_type=MESH)
 
-    def store(base, c):
-        at = row_at(base, c)
-        return pltpu.make_async_copy(staged.at[at, :], out.at[at, :], store_sem.at[base // half, c])
+    for copy in load(0, 0):
+        copy.start()
+
+    barrier = pltpu.get_barrier_semaphore()
+    for axis, bit in steps:
+        pl.semaphore_signal(barrier, inc=1, device_id={axis: peer_of(axis, bit)}, device_id_type=MESH)
 
     for side in range(2):
-        @pl.loop(0, pieces)
+        @pl.loop(1 - side, pieces)
         def _(c):
             for copy in load(side, c):
                 copy.start()
-
-    barrier = pltpu.get_barrier_semaphore()
-    for axis, bit in steps:
-        pl.semaphore_signal(barrier, inc=1, device_id={axis: peer_of(axis, bit)}, device_id_type=MESH)
 
     squares[...] = jnp.zeros_like(squares)
     merged_squares[...] = jnp.zeros_like(merged_squares)
@@ -103,8 +102,10 @@
 
     partial(0, 0, sent)
     pl.semaphore_wait(barrier, len(steps))
-
-    @pl.loop(1, pieces)
+    send(0).start()
+    partial(0, 1, sent)
+
+    @pl.loop(2, pieces)
     def _(c):
         partial(0, c, sent)
         send(c - 1).start()
@@ -158,8 +159,7 @@
         at = row_at(mine_base, c)
         for start, width in blocks:
             span = pl.ds(start, width)
-            staged[at, span] = merged[c, :, span] * rescale
-        store(mine_base, c).start()
+            out[at, span] = merged[c, :, span] * rescale
 
     @pl.loop(0, pieces)
     def _(c):
@@ -167,8 +167,7 @@
         at = row_at(other_base, c)
         for start, width in blocks:
             span = pl.ds(start, width)
-            staged[at, span] = reply[c, :, span] * rescale
-        store(other_base, c).start()
+            out[at, span] = reply[c, :, span] * rescale
 
     for s in range(len(steps)):
         exchange(s).wait_send()
@@ -177,8 +176,6 @@
     def _(c):
         send(c).wait_send()
         answer(c).wait_send()
-        store(mine_base, c).wait()
-        store(other_base, c).wait()
 
 
 def shards(mesh, deltas, fishers):
@@ -192,9 +189,9 @@
     dma = pltpu.SemaphoreType.DMA
     return pl.pallas_call(
         functools.partial(kernel, steps, tasks),
-        out_shape=jax.ShapeDtypeStruct((rows, cols), f32),
-        in_specs=[pl.BlockSpec(memory_space=pl.ANY)] * 2,
-        out_specs=pl.BlockSpec(memory_space=pl.ANY),
+        out_shape=pltpu.VMEM((rows, cols), f32),
+        in_specs=[pl.BlockSpec(memory_space=pltpu.HBM)] * 2,
+        out_specs=pl.BlockSpec(memory_space=pltpu.VMEM),
         scratch_shapes=[
             pltpu.VMEM(deltas.shape, deltas.dtype),
             pltpu.VMEM(fishers.shape, fishers.dtype),
@@ -203,7 +200,6 @@
             pltpu.VMEM((pieces, 2, ROW_STEP, cols), f32),
             pltpu.VMEM((pieces, ROW_STEP, cols), f32),
             pltpu.VMEM((pieces, ROW_STEP, cols), f32),
-            pltpu.VMEM((rows, cols), f32),
             pltpu.VMEM((held, ROW_STEP, cols), f32),
             pltpu.VMEM((ROW_STEP, cols), f32),
             pltpu.VMEM((len(steps), sum_rows, 128), f32),
@@ -215,11 +211,10 @@
             dma((pieces,)),
             dma((len(steps),)),
             dma((len(steps),)),
-            dma((2, pieces)),
         ],
-        compiler_params=pltpu.CompilerParams(collective_id=0, has_side_effects=True),
+        compiler_params=pltpu.CompilerParams(collective_id=0, has_side_effects=True, vmem_limit_bytes=32 * 1024 * 1024),
         name="merge",
-    )(deltas, fishers)
+    )(*(pltpu.with_memory_space_constraint(x, pltpu.HBM) for x in (deltas, fishers)))
 
 
 def solution(mesh):

time: 87 us -> 84.2 us (0.968)
  local copies, waits for them, and re-layouts: 3.22 us -> 1.41 us
  Pallas kernels: 83.6 us -> 82.6 us
    unnamed x1, local copies, waits for them, and re-layouts: 3.22 us -> 1.41 us
    pallas_call x1, Pallas kernels: 83.6 us -> 82.6 us  [shards(): pl.pallas_call(functools.partial(kernel, steps, tasks), out_shape=pltpu.V...]
where the time goes in v2:
time: 84.2 us; the launch traced here: 84 us
  Pallas kernels  82.6 us (98%)
  local copies, waits for them, and re-layouts  1.41 us (2%)
    pallas_call x1, Pallas kernels, shards(): pl.pallas_call(functools.partial(kernel, steps, tasks), out_shape=pltpu.V...  82.6 us

profile of v2, /device:TPU:0, one launch (start us, length us, event | category | flops | bytes accessed | tf_op | source)
XLA Modules:
  0.0 84.0 jit_solution(3387866098804999989)
XLA Ops:
  0.0 82.6 %merge.1 = f32[256,2304]{1,0:T(8,128)S(1)} custom-call(bf16[3,256,2304]{2,1,0:T(8,128)(2,1)} %deltas.1, bf16[3,256,2304]{2,1,0:T(8,128)(2,1)} %fishers.1), custom_call_target="tpu_custom_call" | custom-call | tf_op jit(solution)/shard_map/merge/pallas_call | solution.py:190
  82.6 1.4 %copy.4 = f32[256,2304]{1,0:T(8,128)} copy(f32[256,2304]{1,0:T(8,128)S(1)} %merge.1) | data formatting | bytes 4718592

commit v3 on v2

--- a/solution.py
+++ b/solution.py
@@ -10,13 +10,13 @@
 MESH = pl.DeviceIdType.MESH
 ROW_STEP = 16
 COL_STEP = 256
+CORES = 2
 EARLY_REPLIES = 2
 
 
 def exchange_steps(mesh):
     steps = []
-    for axis in ("task", "mp", "dp"):
-        size = mesh.shape[axis]
+    for axis, size in (("task", mesh.shape["task"]), ("mp", mesh.shape["mp"]), ("dp", CORES)):
         assert size & (size - 1) == 0
         bit = 1
         while bit < size:
@@ -30,9 +30,10 @@
     return me + bit - 2 * bit * (me // bit % 2)
 
 
-def kernel(steps, tasks, deltas, fishers, out, delta_v, fisher_v, sent, own, landed, merged, reply,
+def kernel(steps, chips, tasks, deltas, fishers, out, delta_v, fisher_v, sent, own, landed, merged, reply,
            squares, merged_squares, sums, sums_in, load_sem, send_sem, recv_sem, reply_send, reply_recv,
-           sum_send, sum_recv):
+           sum_send, sum_recv,
+           line, line_in, line_send, line_recv, head_load, head_send, head_recv):
     held, rows, cols = delta_v.shape
     half = rows // 2
     pieces = half // ROW_STEP
@@ -62,18 +63,53 @@
             src_ref=merged.at[c], dst_ref=reply.at[c], send_sem=reply_send.at[c], recv_sem=reply_recv.at[c],
             device_id=partner, device_id_type=MESH)
 
+    first = 2 * COL_STEP if cols > 2 * COL_STEP and cols % 128 == 0 else cols
+    parts = [(0, first)] + ([(first, cols - first)] if first < cols else [])
+
+    def head_loads(p):
+        at = row_at(other_base, 0)
+        span = pl.ds(*parts[p])
+        return (
+            pltpu.make_async_copy(deltas.at[:, at, span], delta_v.at[:, at, span], head_load.at[0, p]),
+            pltpu.make_async_copy(fishers.at[:, at, span], fisher_v.at[:, at, span], head_load.at[1, p]),
+        )
+
+    def send_head(p):
+        span = pl.ds(*parts[p])
+        return pltpu.make_async_remote_copy(
+            src_ref=sent.at[0, :, :, span], dst_ref=landed.at[0, :, :, span], send_sem=head_send.at[p],
+            recv_sem=head_recv.at[p], device_id=partner, device_id_type=MESH)
+
+    row = lax.axis_index("dp")
+    chip = row // CORES
+    has_next = (jnp.bool_(True), chip < chips - 1, chip > 0)
+
+    def pass_on(way):
+        to = lax.rem(row + way * CORES + chips * CORES, chips * CORES)
+        slot = 0 if way == 1 else 1
+        return pltpu.make_async_remote_copy(
+            src_ref=line.at[slot], dst_ref=line_in.at[slot], send_sem=line_send.at[slot],
+            recv_sem=line_recv.at[slot], device_id={"dp": to}, device_id_type=MESH)
+
     def exchange(s):
         axis, bit = steps[s]
         return pltpu.make_async_remote_copy(
             src_ref=sums.at[s], dst_ref=sums_in.at[s], send_sem=sum_send.at[s], recv_sem=sum_recv.at[s],
             device_id={axis: peer_of(axis, bit)}, device_id_type=MESH)
 
-    for copy in load(0, 0):
-        copy.start()
+    line_in[...] = jnp.zeros_like(line_in)
+    for p in range(len(parts)):
+        for copy in head_loads(p):
+            copy.start()
 
     barrier = pltpu.get_barrier_semaphore()
     for axis, bit in steps:
         pl.semaphore_signal(barrier, inc=1, device_id={axis: peer_of(axis, bit)}, device_id_type=MESH)
+    for way in (1, -1):
+        @pl.when(has_next[way])
+        def _():
+            pl.semaphore_signal(
+                barrier, inc=1, device_id={"dp": row + way * CORES}, device_id_type=MESH)
 
     for side in range(2):
         @pl.loop(1 - side, pieces)
@@ -87,8 +123,11 @@
     def partial(side, c, target):
         for copy in load(side, c):
             copy.wait()
+        combine(side, c, target, blocks)
+
+    def combine(side, c, target, chosen):
         at = row_at(other_base if side == 0 else mine_base, c)
-        for start, width in blocks:
+        for start, width in chosen:
             span = pl.ds(start, width)
             numerator = denominator = None
             for k in range(held):
@@ -100,10 +139,16 @@
             target[c, 0, :, span] = numerator
             target[c, 1, :, span] = denominator
 
-    partial(0, 0, sent)
-    pl.semaphore_wait(barrier, len(steps))
-    send(0).start()
+    for p, (low, size) in enumerate(parts):
+        for copy in head_loads(p):
+            copy.wait()
+        combine(0, 0, sent, [block for block in blocks if low <= block[0] < low + size])
+        if p == 0:
+            pl.semaphore_wait(barrier, len(steps) + has_next[1].astype(jnp.int32) + has_next[-1].astype(jnp.int32))
+            send_head(0).start()
     partial(0, 1, sent)
+    for p in range(1, len(parts)):
+        send_head(p).start()
 
     @pl.loop(2, pieces)
     def _(c):
@@ -118,17 +163,19 @@
         partial(1, c, own)
 
     def merge(c):
-        send(c).wait_recv()
         for start, width in blocks:
             span = pl.ds(start, width)
             value = (own[c, 0, :, span] + landed[c, 0, :, span]) / (own[c, 1, :, span] + landed[c, 1, :, span])
             merged[c, :, span] = value
             merged_squares[:, span] += value * value
 
+    for p in range(len(parts)):
+        send_head(p).wait_recv()
     merge(0)
 
     @pl.loop(1, pieces)
     def _(c):
+        send(c).wait_recv()
         merge(c)
 
         @pl.when(c <= EARLY_REPLIES)
@@ -149,6 +196,29 @@
         exchange(s).wait_recv()
         totals = totals + sums_in[s]
 
+    def sweep(way):
+        slot = 0 if way == 1 else 1
+
+        @pl.when(has_next[-way])
+        def _():
+            pass_on(way).wait_recv()
+
+        @pl.when(has_next[way])
+        def _():
+            line[slot] = line_in[slot] + totals
+            pass_on(way).start()
+
+    @pl.when(chip < chips // 2)
+    def _():
+        sweep(1)
+        sweep(-1)
+
+    @pl.when(chip >= chips // 2)
+    def _():
+        sweep(-1)
+        sweep(1)
+
+    totals = totals + line_in[0] + line_in[1]
     roots = jnp.sqrt(totals + 1e-06)
     target = jnp.sum(jnp.where(index < tasks, roots, 0.0), axis=0, keepdims=True) / tasks
     norm = jnp.sum(jnp.where(index == tasks, roots, 0.0), axis=0, keepdims=True)
@@ -172,10 +242,21 @@
     for s in range(len(steps)):
         exchange(s).wait_send()
 
+    for way in (1, -1):
+        @pl.when(has_next[way])
+        def _():
+            pass_on(way).wait_send()
+
+    for p in range(len(parts)):
+        send_head(p).wait_send()
+
     @pl.loop(0, pieces)
     def _(c):
-        send(c).wait_send()
         answer(c).wait_send()
+
+        @pl.when(c > 0)
+        def _():
+            send(c).wait_send()
 
 
 def shards(mesh, deltas, fishers):
@@ -188,7 +269,7 @@
     f32 = jnp.float32
     dma = pltpu.SemaphoreType.DMA
     return pl.pallas_call(
-        functools.partial(kernel, steps, tasks),
+        functools.partial(kernel, steps, mesh.shape["dp"] // CORES, tasks),
         out_shape=pltpu.VMEM((rows, cols), f32),
         in_specs=[pl.BlockSpec(memory_space=pltpu.HBM)] * 2,
         out_specs=pl.BlockSpec(memory_space=pltpu.VMEM),
@@ -211,6 +292,13 @@
             dma((pieces,)),
             dma((len(steps),)),
             dma((len(steps),)),
+            pltpu.VMEM((2, sum_rows, 128), f32),
+            pltpu.VMEM((2, sum_rows, 128), f32),
+            dma((2,)),
+            dma((2,)),
+            dma((2, 2)),
+            dma((2,)),
+            dma((2,)),
         ],
         compiler_params=pltpu.CompilerParams(collective_id=0, has_side_effects=True, vmem_limit_bytes=32 * 1024 * 1024),
         name="merge",

time: 84.2 us -> 83.2 us (0.988)
  Pallas kernels: 82.6 us -> 81.7 us
    pallas_call x1, Pallas kernels: 82.6 us -> 81.7 us  [shards(): pl.pallas_call(functools.partial(kernel, steps, mesh.shape['dp'] // CORES...]
where the time goes in v3:
time: 83.2 us; the launch traced here: 83.1 us
  Pallas kernels  81.7 us (98%)
  local copies, waits for them, and re-layouts  1.41 us (2%)
    pallas_call x1, Pallas kernels, shards(): pl.pallas_call(functools.partial(kernel, steps, mesh.shape['dp'] // CORES...  81.7 us

profile of v3, /device:TPU:0, one launch (start us, length us, event | category | flops | bytes accessed | tf_op | source)
XLA Modules:
  0.0 83.1 jit_solution(6374096774866982881)
XLA Ops:
  0.0 81.7 %merge.1 = f32[256,2304]{1,0:T(8,128)S(1)} custom-call(bf16[3,256,2304]{2,1,0:T(8,128)(2,1)} %deltas.1, bf16[3,256,2304]{2,1,0:T(8,128)(2,1)} %fishers.1), custom_call_target="tpu_custom_call" | custom-call | tf_op jit(solution)/shard_map/merge/pallas_call | solution.py:271
  81.7 1.4 %copy.4 = f32[256,2304]{1,0:T(8,128)} copy(f32[256,2304]{1,0:T(8,128)S(1)} %merge.1) | data formatting | bytes 4718592

commit v4 on v3

--- a/solution.py
+++ b/solution.py
@@ -30,10 +30,15 @@
     return me + bit - 2 * bit * (me // bit % 2)
 
 
+def strip_cut(cols):
+    return cols * 2 // 3 // COL_STEP * COL_STEP if cols >= 3 * COL_STEP and cols % 128 == 0 else cols
+
+
 def kernel(steps, chips, tasks, deltas, fishers, out, delta_v, fisher_v, sent, own, landed, merged, reply,
            squares, merged_squares, sums, sums_in, load_sem, send_sem, recv_sem, reply_send, reply_recv,
            sum_send, sum_recv,
-           line, line_in, line_send, line_recv, head_load, head_send, head_recv):
+           line, line_in, line_send, line_recv, head_load, head_send, head_recv,
+           strip_in=None, strip_merged=None, strip_reply=None, strip_send=None, strip_recv=None):
     held, rows, cols = delta_v.shape
     half = rows // 2
     pieces = half // ROW_STEP
@@ -79,6 +84,37 @@
         return pltpu.make_async_remote_copy(
             src_ref=sent.at[0, :, :, span], dst_ref=landed.at[0, :, :, span], send_sem=head_send.at[p],
             recv_sem=head_recv.at[p], device_id=partner, device_id_type=MESH)
+
+    last = pieces - 1
+    cut = strip_cut(cols)
+    strip = cols - cut
+    low, high = pl.ds(0, cut), pl.ds(cut, strip)
+    low_blocks = [block for block in blocks if block[0] < cut]
+    leading = me == 0
+
+    def roles(of_leading, of_other):
+        pl.when(leading)(of_leading)
+        pl.when(jnp.logical_not(leading))(of_other)
+
+    def send_low():
+        return pltpu.make_async_remote_copy(
+            src_ref=sent.at[last, :, :, low], dst_ref=landed.at[last, :, :, low], send_sem=send_sem.at[last],
+            recv_sem=recv_sem.at[last], device_id=partner, device_id_type=MESH)
+
+    def answer_low():
+        return pltpu.make_async_remote_copy(
+            src_ref=merged.at[last, :, low], dst_ref=reply.at[last, :, low], send_sem=reply_send.at[last],
+            recv_sem=reply_recv.at[last], device_id=partner, device_id_type=MESH)
+
+    def send_strip():
+        return pltpu.make_async_remote_copy(
+            src_ref=own.at[last, :, :, high], dst_ref=strip_in, send_sem=strip_send.at[0],
+            recv_sem=strip_recv.at[0], device_id=partner, device_id_type=MESH)
+
+    def answer_strip():
+        return pltpu.make_async_remote_copy(
+            src_ref=strip_merged, dst_ref=strip_reply, send_sem=strip_send.at[1],
+            recv_sem=strip_recv.at[1], device_id=partner, device_id_type=MESH)
 
     row = lax.axis_index("dp")
     chip = row // CORES
@@ -139,10 +175,10 @@
             target[c, 0, :, span] = numerator
             target[c, 1, :, span] = denominator
 
-    for p, (low, size) in enumerate(parts):
+    for p, (begin, size) in enumerate(parts):
         for copy in head_loads(p):
             copy.wait()
-        combine(0, 0, sent, [block for block in blocks if low <= block[0] < low + size])
+        combine(0, 0, sent, [block for block in blocks if begin <= block[0] < begin + size])
         if p == 0:
             pl.semaphore_wait(barrier, len(steps) + has_next[1].astype(jnp.int32) + has_next[-1].astype(jnp.int32))
             send_head(0).start()
@@ -156,14 +192,19 @@
         send(c - 1).start()
 
     partial(1, 0, own)
-    send(pieces - 1).start()
+    roles(lambda: send(last).start(), lambda: send_low().start())
 
     @pl.loop(1, pieces)
     def _(c):
         partial(1, c, own)
 
-    def merge(c):
-        for start, width in blocks:
+    if strip:
+        @pl.when(leading)
+        def _():
+            send_strip().start()
+
+    def merge(c, chosen=blocks):
+        for start, width in chosen:
             span = pl.ds(start, width)
             value = (own[c, 0, :, span] + landed[c, 0, :, span]) / (own[c, 1, :, span] + landed[c, 1, :, span])
             merged[c, :, span] = value
@@ -173,7 +214,7 @@
         send_head(p).wait_recv()
     merge(0)
 
-    @pl.loop(1, pieces)
+    @pl.loop(1, last)
     def _(c):
         send(c).wait_recv()
         merge(c)
@@ -181,6 +222,21 @@
         @pl.when(c <= EARLY_REPLIES)
         def _():
             answer(c - 1).start()
+
+    def merge_low():
+        send_low().wait_recv()
+        merge(last, low_blocks)
+
+    def merge_last():
+        send(last).wait_recv()
+        merge(last)
+        if strip:
+            send_strip().wait_recv()
+            value = (sent[last, 0, :, high] + strip_in[0]) / (sent[last, 1, :, high] + strip_in[1])
+            strip_merged[...] = value
+            merged_squares[:, high] += value * value
+
+    roles(merge_low, merge_last)
 
     index = lax.broadcasted_iota(jnp.int32, sums.shape[1:], 0)
     totals = jnp.where(index == tasks, jnp.sum(merged_squares[...]), 0.0)
@@ -190,9 +246,16 @@
         sums[s] = totals
         exchange(s).start()
         if s == 0:
-            @pl.loop(EARLY_REPLIES, pieces)
+            @pl.loop(EARLY_REPLIES, last)
             def _(c):
                 answer(c).start()
+
+            def answer_last():
+                answer(last).start()
+                if strip:
+                    answer_strip().start()
+
+            roles(lambda: answer_low().start(), answer_last)
         exchange(s).wait_recv()
         totals = totals + sums_in[s]
 
@@ -224,20 +287,47 @@
     norm = jnp.sum(jnp.where(index == tasks, roots, 0.0), axis=0, keepdims=True)
     rescale = jnp.max(target / norm)
 
-    @pl.loop(0, pieces)
-    def _(c):
-        at = row_at(mine_base, c)
-        for start, width in blocks:
+    def scale(source, base, c, chosen=blocks):
+        at = row_at(base, c)
+        for start, width in chosen:
             span = pl.ds(start, width)
-            out[at, span] = merged[c, :, span] * rescale
-
-    @pl.loop(0, pieces)
+            out[at, span] = source[c, :, span] * rescale
+
+    @pl.loop(0, last)
+    def _(c):
+        scale(merged, mine_base, c)
+
+    def scale_last():
+        scale(merged, mine_base, last)
+        if strip:
+            out[row_at(other_base, last), high] = strip_merged[...] * rescale
+
+    roles(lambda: scale(merged, mine_base, last, low_blocks), scale_last)
+
+    @pl.loop(0, last)
     def _(c):
         answer(c).wait_recv()
-        at = row_at(other_base, c)
-        for start, width in blocks:
-            span = pl.ds(start, width)
-            out[at, span] = reply[c, :, span] * rescale
+        scale(reply, other_base, c)
+
+    def finish():
+        answer(last).wait_recv()
+        scale(reply, other_base, last)
+        send(last).wait_send()
+        answer_low().wait_send()
+        if strip:
+            answer_strip().wait_recv()
+            out[row_at(mine_base, last), high] = strip_reply[...] * rescale
+            send_strip().wait_send()
+
+    def finish_other():
+        answer_low().wait_recv()
+        scale(reply, other_base, last, low_blocks)
+        send_low().wait_send()
+        answer(last).wait_send()
+        if strip:
+            answer_strip().wait_send()
+
+    roles(finish, finish_other)
 
     for s in range(len(steps)):
         exchange(s).wait_send()
@@ -250,7 +340,7 @@
     for p in range(len(parts)):
         send_head(p).wait_send()
 
-    @pl.loop(0, pieces)
+    @pl.loop(0, last)
     def _(c):
         answer(c).wait_send()
 
@@ -268,6 +358,14 @@
     sum_rows = (tasks + 8) // 8 * 8
     f32 = jnp.float32
     dma = pltpu.SemaphoreType.DMA
+    strip = cols - strip_cut(cols)
+    strip_scratch = [
+        pltpu.VMEM((2, ROW_STEP, strip), f32),
+        pltpu.VMEM((ROW_STEP, strip), f32),
+        pltpu.VMEM((ROW_STEP, strip), f32),
+        dma((2,)),
+        dma((2,)),
+    ] if strip else []
     return pl.pallas_call(
         functools.partial(kernel, steps, mesh.shape["dp"] // CORES, tasks),
         out_shape=pltpu.VMEM((rows, cols), f32),
@@ -299,7 +397,7 @@
             dma((2, 2)),
             dma((2,)),
             dma((2,)),
-        ],
+        ] + strip_scratch,
         compiler_params=pltpu.CompilerParams(collective_id=0, has_side_effects=True, vmem_limit_bytes=32 * 1024 * 1024),
         name="merge",
     )(*(pltpu.with_memory_space_constraint(x, pltpu.HBM) for x in (deltas, fishers)))

time: 83.2 us -> 82.4 us (level)
  Pallas kernels: 81.7 us -> 80.8 us
    pallas_call x1, Pallas kernels: 81.7 us -> 80.8 us  [shards(): pl.pallas_call(functools.partial(kernel, steps, mesh.shape['dp'] // CORES...]
where the time goes in v4:
time: 82.4 us; the launch traced here: 82.2 us
  Pallas kernels  80.8 us (98%)
  local copies, waits for them, and re-layouts  1.41 us (2%)
    pallas_call x1, Pallas kernels, shards(): pl.pallas_call(functools.partial(kernel, steps, mesh.shape['dp'] // CORES...  80.8 us

profile of v4, /device:TPU:0, one launch (start us, length us, event | category | flops | bytes accessed | tf_op | source)
XLA Modules:
  0.0 82.2 jit_solution(7753003716726456941)
XLA Ops:
  0.0 80.8 %merge.1 = f32[256,2304]{1,0:T(8,128)S(1)} custom-call(bf16[3,256,2304]{2,1,0:T(8,128)(2,1)} %deltas.1, bf16[3,256,2304]{2,1,0:T(8,128)(2,1)} %fishers.1), custom_call_target="tpu_custom_call" | custom-call | tf_op jit(solution)/shard_map/merge/pallas_call | solution.py:369
  80.8 1.4 %copy.4 = f32[256,2304]{1,0:T(8,128)} copy(f32[256,2304]{1,0:T(8,128)S(1)} %merge.1) | data formatting | bytes 4718592
